TPU v7x, 32 devices: a whole 2x2x4 slice. The times are simulated.
32 devices in a mesh: section: 2 (over x), dp: 16 (over z, y, core).
Axes of the slice: x: 2, y: 2, z: 4, core: 2. Of those that a mesh axis runs over, the one named last changes fastest.
Arguments:
- activations: bfloat16 [4, 256, 4608], P('section', 'dp'), may hold values from -6 to 6
- section_sources: int32 [4], replicated, may hold values from 0 to 3, as said below
- accumulators: float32 [256, 4, 4608], P('dp', 'section'), may hold values from -6 to 6
- block_sources: int32 [256], replicated, may hold values from 0 to 255, as said below
- loss_terms: float32 [2, 16], P('section', 'dp'), may hold values from 0.35 to 6
- pre_gain: float32 [2, 4608], P('section'), may hold values from 0.1 to 1.9
- query_weight: bfloat16 [2, 4608, 2048], P('section', None, 'dp'), may hold values from -0.09375 to 0.09375
- keyval_weight: bfloat16 [2, 4608, 2048], P('section', None, 'dp'), may hold values from -0.09375 to 0.09375
- output_weight: bfloat16 [2, 2048, 4608], P('section', 'dp'), may hold values from -0.125 to 0.125
- post_gain: float32 [2, 4608], P('section'), may hold values from 0.1 to 1.9
Outputs:
- new_activations: bfloat16 [4, 256, 4608], P('section', 'dp')
- new_accumulators: float32 [256, 4, 4608], P('dp', 'section')
- check_out: bfloat16 [2, 256, 4608], P('section', 'dp')
Inputs may be any that keep to these rules, and one draw needn't show every extreme that they name: `section_sources`: A permutation; each old section's micro-batches fill 1 slots of each new section. `block_sources`: A permutation; each old data index's blocks fill 1 block of each new data index.
All inputs are finite; a program needn't handle non-finite values.
Results may differ from a plain program's by a relative error of at most 0.014.
Values may be sent and summed in bfloat16 or wider, within the bound.
A program may use at most 64 MiB of HBM per device.

v0:
```python
import jax
import jax.numpy as jnp
from jax import lax
from jax.sharding import PartitionSpec as P

D = 4608


def partner(value, axis, stride):
    mask = 2**stride
    pairs = [(source, source ^ mask) for source in range(lax.axis_size(axis))]
    return lax.ppermute(value, axis, pairs)


def rms_norm(values, gain):
    meansq = jnp.mean(values * values, axis=-1, keepdims=True)
    return values * lax.rsqrt(meansq + 1e-06) * gain


def rotary(values, positions):
    width = values.shape[-1]
    middle = width // 2
    counter = jnp.arange(middle, dtype=jnp.float32)
    freqs = 10000.0 ** (-2.0 * counter / width)
    angles = positions.astype(jnp.float32)[:, None] * freqs[None, :]
    cosine = jnp.cos(angles)
    sine = jnp.sin(angles)
    first = values[..., :middle]
    second = values[..., middle:]
    return jnp.concatenate(
        [first * cosine - second * sine, second * cosine + first * sine], axis=-1
    )


def plan_routes(sources, own_index, groups, per_group):
    per_peer = per_group // groups
    table = sources.reshape(groups, per_group)
    owners = table // per_group
    places = table % per_group
    slot_ids = jnp.arange(per_group, dtype=jnp.int32)
    sort_keys = jnp.where(owners == own_index, slot_ids[None, :], slot_ids[None, :] + per_group)
    ranking = jnp.argsort(sort_keys, axis=1)[:, :per_peer]
    send_index = jnp.take_along_axis(places, ranking, axis=1).reshape(-1)
    my_owners = lax.dynamic_slice_in_dim(owners, own_index, 1, 0)[0]
    earlier = (my_owners[None, :] == my_owners[:, None]) & (slot_ids[None, :] < slot_ids[:, None])
    earlier_count = jnp.sum(earlier.astype(jnp.int32), axis=1)
    recv_index = my_owners * per_peer + earlier_count
    return (send_index, recv_index)


def on_device(
    activations,
    section_sources,
    accumulators,
    block_sources,
    loss_terms,
    pre_gain,
    query_weight,
    keyval_weight,
    output_weight,
    post_gain,
):
    section_index = lax.axis_index("section")
    mb_local = activations.shape[0]
    gathered = lax.all_gather(activations, "section", axis=0, tiled=True)
    my_slots = lax.dynamic_slice_in_dim(section_sources, section_index * mb_local, mb_local)
    moved = jnp.take(gathered, my_slots, axis=0)
    data_ranks = lax.axis_size("dp")
    data_index = lax.axis_index("dp")
    blk_local = accumulators.shape[0]
    per_peer = blk_local // data_ranks
    block_send, block_recv = plan_routes(block_sources, data_index, data_ranks, blk_local)
    outgoing_blocks = jnp.take(accumulators, block_send, axis=0)
    term_rows = jnp.broadcast_to(loss_terms, (blk_local, 1))
    incoming_blocks, incoming_terms = (
        lax.all_to_all(
            outgoing_blocks.astype(jnp.bfloat16), "dp", split_axis=0, concat_axis=0, tiled=True
        ).astype(outgoing_blocks.dtype),
        lax.all_to_all(
            term_rows.astype(jnp.bfloat16), "dp", split_axis=0, concat_axis=0, tiled=True
        ).astype(term_rows.dtype),
    )
    scale_sum = jnp.sum(incoming_terms[::per_peer, 0])
    factor = data_ranks / scale_sum
    new_accumulators = jnp.take(incoming_blocks, block_recv, axis=0) * factor
    checked = moved[0]
    head_size = query_weight.shape[2]
    is_even = data_index % 2 == 0
    w_query = query_weight[0]
    w_keyval = keyval_weight[0]
    gain_pre = pre_gain[0]
    block_rows = lax.all_gather(checked, "dp", axis=0, tiled=True)
    row_count = block_rows.shape[0]
    positions = jnp.arange(row_count, dtype=jnp.int32)
    normed = rms_norm(block_rows.astype(jnp.float32), gain_pre).astype(jnp.bfloat16)
    queries = jnp.dot(normed, w_query, preferred_element_type=jnp.float32)
    own_proj = jnp.dot(normed, w_keyval, preferred_element_type=jnp.float32)
    queries = rotary(queries, positions)
    own_proj = jnp.where(is_even, rotary(own_proj, positions), own_proj)
    projected = jnp.concatenate([queries, own_proj], axis=1).astype(jnp.bfloat16)
    queries = projected[:, :head_size]
    own_kv = projected[:, head_size:]
    partner_kv = partner(own_kv, "dp", 0)
    key_rows = jnp.where(is_even, own_kv, partner_kv)
    value_rows = jnp.where(is_even, partner_kv, own_kv)
    length = projected.shape[0]
    positions = jnp.arange(length, dtype=jnp.int32)
    scale_factor = (D / data_ranks) ** (-0.5)
    scores = (
        lax.dot_general(
            queries, key_rows, (((1,), (1,)), ((), ())), preferred_element_type=jnp.float32
        )
        * scale_factor
    )
    capped = 50.0 * jnp.tanh(scores / 50.0)
    causal = positions[None, :] <= positions[:, None]
    expd = jnp.where(causal, jnp.exp(capped), 0.0)
    denominator = jnp.sum(expd, axis=-1, keepdims=True)
    probs = expd.astype(jnp.bfloat16)
    numer = jnp.dot(probs, value_rows, preferred_element_type=jnp.float32)
    attended = (numer / denominator).astype(jnp.bfloat16)
    w_output = output_weight[0]
    summed = lax.psum_scatter(
        jnp.dot(attended, w_output, preferred_element_type=jnp.float32).astype(jnp.bfloat16),
        "dp",
        scatter_dimension=0,
        tiled=True,
    ).astype(jnp.float32)
    check_out = (checked.astype(jnp.float32) + rms_norm(summed, post_gain[0])).astype(jnp.bfloat16)
    return (moved, new_accumulators, check_out[None, :, :])


def solution(mesh):
    placed = (
        P("section", "dp", None),
        P(),
        P("dp", "section", None),
        P(),
        P("section", "dp"),
        P("section", None),
        P("section", None, "dp"),
        P("section", None, "dp"),
        P("section", "dp", None),
        P("section", None),
    )
    return jax.shard_map(
        on_device,
        mesh=mesh,
        in_specs=placed,
        out_specs=(P("section", "dp", None), P("dp", "section", None), P("section", "dp", None)),
        check_vma=False,
    )
```

profile of v0, /device:TPU:0, one launch (start us, length us, event | category | flops | bytes accessed | tf_op | source)
XLA Modules:
  0.0 145.7 jit_solution(12692090813205101284)
XLA Ops:
  7.3 0.8 compare_and_fusion.2
  8.1 10.9 %all_gather.6 = bf16[4,16,4608]{2,1,0:T(8,128)(2,1)S(1)} all-gather(bf16[2,16,4608]{2,1,0:T(8,128)(2,1)} %param.12), channel_id=1, replica_groups=mesh['section'=2,'dp'=16] {'section'}, dimensions={0}, use_global_device_ids=true | all-gather | bytes 884736 | tf_op jit(solution)/shard_map/all_gather | solution.py:65
  19.0 0.6 gather_fusion
  19.7 0.7 slice.38
  21.1 0.6 broadcast_in_dim.70
  21.7 6.1 %all-to-all-start.1 = ((bf16[16,1,1]{2,1,0:T(2,128)(2,1)}), bf16[16,1,1]{2,1,0:T(2,128)(2,1)S(1)}, u32[]{:S(2)}, u32[]{:S(2)}) async-start(bf16[16,1,1]{2,1,0:T(2,128)(2,1)} %broadcast_in_dim.70), calls=%async_computation.1 | async-start | bytes 16384 | tf_op jit(solution)/shard_map/all_to_all | solution.py:79
  28.1 0.7 sort.17
  28.9 35.5 %all-gather.3.cloned.1.call-done = bf16[1,256,4608]{2,1,0:T(8,128)(2,1)} async-done(((bf16[1,16,4608]{2,1,0:T(8,128)(2,1)}), bf16[1,256,4608]{2,1,0:T(8,128)(2,1)}) %all-gather.3.cloned.1.call-update) | async-done | bytes 2359312 | tf_op jit(solution)/shard_map/all_gather | solution.py:92
  64.4 2.4 %fusion = f32[256]{0:T(256)S(1)} fusion(bf16[1,256,4608]{2,1,0:T(8,128)(2,1)} %all-gather.3.cloned.1.call-done), kind=kLoop, calls=%fused_computation.7 | loop fusion | flops 3538688 | bytes 2360320 | tf_op jit(solution)/shard_map/reduce_sum | solution.py:16
  66.8 2.4 %fusion.4 = f32[256,128]{0,1:T(8,128)S(1)} fusion(bf16[1,4608,128]{2,1,0:T(8,128)(2,1)} %param.19, bf16[1,256,4608]{2,1,0:T(8,128)(2,1)S(1)} %copy-done.1, f32[4608]{0:T(1024)S(1)} %reduce.1, f32[256]{0:T(256)S(1)} %add_rsqrt_fusion), kind=kOutput, calls=%fused_computation.11 | convolution fusion | flops 306708480 | bytes 3689472 | tf_op jit(solution)/shard_map/dot_general | solution.py:97
  69.2 0.3 fusion.35
  69.8 1.1 fusion.6
  71.6 2.4 %convolution_convert_fusion = bf16[256,4608]{1,0:T(8,128)(2,1)} fusion(bf16[1,128,4608]{2,1,0:T(8,128)(2,1)S(1)} %copy-done, bf16[256,256]{0,1:T(8,128)(2,1)S(1)} %get-tuple-element.20, f32[256]{0:T(256)S(1)} %get-tuple-element.19, bf16[256,128]{0,1:T(8,128)(2,1)S(1)} %collective-permute-done, bf16[256,128]{0,1:T(8,128)(2,1)S(1)} %fusion.20, pred[]{:T(512)S(6)} %eq.31), kind=kOutput, calls=%fused_computation.4 | convolution fusion | flops 320045056 | bytes 3802113 | tf_op jit(solution)/shard_map/dot_general | solution.py:124
  74.0 0.7 gather_fusion.1
  75.0 1.2 gather_fusion.2
  76.2 1.0 select_convert_fusion
  77.3 3.6 %all-to-all-start = ((bf16[16,2,4608]{2,1,0:T(2,128)(2,1)}), bf16[16,2,4608]{2,1,0:T(2,128)(2,1)S(1)}, u32[]{:S(2)}, u32[]{:S(2)}) async-start(bf16[16,2,4608]{2,1,0:T(2,128)(2,1)} %select_convert_fusion), calls=%async_computation | async-start | bytes 589824 | tf_op jit(solution)/shard_map/all_to_all | solution.py:76
  81.2 0.6 convert_reduce_fusion.1
  82.5 8.9 %all-to-all-done = bf16[16,2,4608]{2,1,0:T(2,128)(2,1)S(1)} async-done(((bf16[16,2,4608]{2,1,0:T(2,128)(2,1)}), bf16[16,2,4608]{2,1,0:T(2,128)(2,1)S(1)}, u32[]{:S(2)}, u32[]{:S(2)}) %all-to-all-start) | async-done | bytes 294944 | tf_op jit(solution)/shard_map/all_to_all | solution.py:76
  91.6 1.2 gather_fusion.3
  92.8 1.1 select_multiply_fusion
  93.9 42.2 %reduce-scatter.2.cloned.1.call-done = bf16[16,4608]{1,0:T(8,128)(2,1)} async-done(((bf16[256,4608]{1,0:T(8,128)(2,1)}), bf16[16,4608]{1,0:T(8,128)(2,1)}) %reduce-scatter.2.cloned.1.call-update) | async-done | bytes 147472 | tf_op jit(solution)/shard_map/reduce_scatter | solution.py:123
  136.1 1.1 fusion.15
  137.1 1.7 %fusion.19 = bf16[1,16,4608]{2,1,0:T(8,128)(2,1)} fusion(bf16[16,4608]{1,0:T(8,128)(2,1)} %reduce-scatter.2.cloned.1.call-done, f32[4608]{0:T(1024)S(1)} %reduce.2, f32[16]{0:T(128)S(1)} %add_rsqrt_fusion.1, bf16[2,16,4608]{2,1,0:T(8,128)(2,1)S(1)} %broadcast_select_fusion), kind=kLoop, calls=%fused_computation.32 | loop fusion | flops 442368 | bytes 460864 | tf_op jit(solution)/shard_map/broadcast_in_dim | solution.py:130
  (51 shorter events, 2.3 us)
Async XLA Ops:
  7.2 64.4 %copy-start = (bf16[1,128,4608]{2,1,0:T(8,128)(2,1)S(1)}, bf16[1,128,4608]{2,1,0:T(8,128)(2,1)}, u32[]{:S(2)}) copy-start(bf16[1,128,4608]{2,1,0:T(8,128)(2,1)} %param.20) | copy-start | bytes 3538948
  7.2 20.7 %copy-start.6 = (s32[256]{0:T(256)S(1)}, s32[256]{0:T(256)}, u32[]{:S(2)}) copy-start(s32[256]{0:T(256)} %param.15) | copy-start | bytes 3076
  7.2 20.9 %copy-start.4 = (f32[1,4608]{1,0:T(1,128)S(1)}, f32[1,4608]{1,0:T(1,128)}, u32[]{:S(2)}) copy-start(f32[1,4608]{1,0:T(1,128)} %param.17) | copy-start | bytes 55300
  7.2 57.2 %all-gather.3.cloned.1.call-start = ((), (), s32[]{:S(2)}) async-start(), calls=%async_computation.4 | async-start | bytes 2506752 | tf_op jit(solution)/shard_map/all_gather | solution.py:92
  19.7 117.5 %copy-start.2 = (bf16[2,16,4608]{2,1,0:T(8,128)(2,1)}, bf16[2,16,4608]{2,1,0:T(8,128)(2,1)S(1)}, u32[]{:S(2)}) copy-start(bf16[2,16,4608]{2,1,0:T(8,128)(2,1)S(1)} %broadcast_select_fusion) | copy-start | bytes 884740
  21.7 55.6 %all-to-all-start.1 = ((bf16[16,1,1]{2,1,0:T(2,128)(2,1)}), bf16[16,1,1]{2,1,0:T(2,128)(2,1)S(1)}, u32[]{:S(2)}, u32[]{:S(2)}) async-start(bf16[16,1,1]{2,1,0:T(2,128)(2,1)} %broadcast_in_dim.70), calls=%async_computation.1 | async-start | bytes 16384 | tf_op jit(solution)/shard_map/all_to_all | solution.py:79
  27.8 108.3 %reduce-scatter.2.cloned.1.call-start = ((), (), s32[]{:S(2)}) async-start(), calls=%async_computation.3 | async-start | bytes 2506752 | tf_op jit(solution)/shard_map/reduce_scatter | solution.py:123
  64.4 2.4 %copy-start.1 = (bf16[1,256,4608]{2,1,0:T(8,128)(2,1)S(1)}, bf16[1,256,4608]{2,1,0:T(8,128)(2,1)}, u32[]{:S(2)}) copy-start(bf16[1,256,4608]{2,1,0:T(8,128)(2,1)} %all-gather.3.cloned.1.call-done) | copy-start | bytes 7077892
  66.8 3.1 %copy-start.7 = (bf16[1,4608,128]{2,1,0:T(8,128)(2,1)S(1)}, bf16[1,4608,128]{2,1,0:T(8,128)(2,1)}, u32[]{:S(2)}) copy-start(bf16[1,4608,128]{2,1,0:T(8,128)(2,1)} %param.18) | copy-start | bytes 3538948
  69.5 1.7 %collective-permute-start = (bf16[256,128]{0,1:T(8,128)(2,1)S(1)}, bf16[256,128]{0,1:T(8,128)(2,1)S(1)}, u32[]{:S(2)}, u32[]{:S(2)}) collective-permute-start(bf16[256,128]{0,1:T(8,128)(2,1)S(1)} %fusion.20), channel_id=1, source_target_pairs={{0,1},{1,0},{2,3},{3,2},{4,5},{5,4},{6,7},{7,6},{8,9},{9,8},{10,11... | collective-permute-start | bytes 196616 | tf_op jit(solution)/shard_map/ppermute | solution.py:12
  74.0 1.1 copy-start.3
  74.0 3.3 %copy-start.5 = (f32[1,4608]{1,0:T(1,128)S(1)}, f32[1,4608]{1,0:T(1,128)}, u32[]{:S(2)}) copy-start(f32[1,4608]{1,0:T(1,128)} %param.21) | copy-start | bytes 55300
  77.3 14.1 %all-to-all-start = ((bf16[16,2,4608]{2,1,0:T(2,128)(2,1)}), bf16[16,2,4608]{2,1,0:T(2,128)(2,1)S(1)}, u32[]{:S(2)}, u32[]{:S(2)}) async-start(bf16[16,2,4608]{2,1,0:T(2,128)(2,1)} %select_convert_fusion), calls=%async_computation | async-start | bytes 589824 | tf_op jit(solution)/shard_map/all_to_all | solution.py:76
Sparse Core Ops, SparseCore 0:
  20.5 43.7 all-gather.2
  74.1 61.9 reduce-scatter.1
where the time goes:
time: 146 us
  waiting for transfers between devices  86.6 us (59%)
  between operations  15.7 us (11%)
  blocking collectives  10.9 us (7%)
  other arithmetic  10.8 us (7%)
  starting transfers between devices  10.1 us (7%)
  matrix products  6.18 us (4%)
  local copies, waits for them, and re-layouts  5.5 us (4%)
    reduce_scatter x1, waiting for transfers between devices, on_device(): lax.psum_scatter(jnp.dot(attended, w_output, preferred_element_type=jnp.f...  42.2 us
    all_gather x1, waiting for transfers between devices, on_device(): block_rows = lax.all_gather(checked, 'dp', axis=0, tiled=True)  35.5 us
    all_gather x1, blocking collectives, on_device(): gathered = lax.all_gather(activations, 'section', axis=0, tiled=True)  10.9 us
    all_to_all x1, waiting for transfers between devices, on_device(): lax.all_to_all(outgoing_blocks.astype(jnp.bfloat16), 'dp', split_axis=0,...  8.9 us
    all_to_all x1, starting transfers between devices, on_device(): lax.all_to_all(term_rows.astype(jnp.bfloat16), 'dp', split_axis=0, concat...  6.13 us
    all_to_all x1, starting transfers between devices, on_device(): lax.all_to_all(outgoing_blocks.astype(jnp.bfloat16), 'dp', split_axis=0,...  3.55 us
    reduce_sum x2, other arithmetic, rms_norm(): meansq = jnp.mean(values * values, axis=-1, keepdims=True)  3.42 us
  transfers between devices with their start and end apart: 5, of which 3 were waited for; matrix products, arithmetic and copies ran while one was open for 12% of the time, Pallas kernels for 0%

commit v1 on v0

--- a/solution.py
+++ b/solution.py
@@ -89,7 +89,14 @@
     w_query = query_weight[0]
     w_keyval = keyval_weight[0]
     gain_pre = pre_gain[0]
-    block_rows = lax.all_gather(checked, "dp", axis=0, tiled=True)
+    size = lax.axis_size("dp")
+    forward = [(i, (i + 1) % size) for i in range(size)]
+    blocks = [checked]
+    for far in range(1, size):
+        blocks = [lax.ppermute(blocks[0], "dp", forward), *blocks]
+    whole = jnp.concatenate(blocks, axis=0)
+    offset = (lax.axis_index("dp") + 1) * blocks[-1].shape[0]
+    block_rows = jnp.roll(whole, offset, axis=0)
     row_count = block_rows.shape[0]
     positions = jnp.arange(row_count, dtype=jnp.int32)
     normed = rms_norm(block_rows.astype(jnp.float32), gain_pre).astype(jnp.bfloat16)

time: 146 us -> 210 us (1.44)
  waiting for transfers between devices: 86.6 us -> 146 us
  other arithmetic: 10.8 us -> 14.1 us
  local copies, waits for them, and re-layouts: 5.5 us -> 8.15 us
    ppermute x0 -> x15, waiting for transfers between devices: none -> 96.8 us  [on_device(): blocks = [lax.ppermute(blocks[0], 'dp', forward), *blocks]]
    all_gather x1 -> x0, waiting for transfers between devices: 35.5 us -> none  [on_device(): block_rows = lax.all_gather(checked, 'dp', axis=0, tiled=True)]
    reduce_scatter x1, waiting for transfers between devices: 42.2 us -> 39.8 us  [on_device(): lax.psum_scatter(jnp.dot(attended, w_output, preferred_element_type=jnp.f...]
  transfers between devices with their start and end apart: 5 -> 19, of which waited for: 3 -> 17; matrix products, arithmetic and copies ran while one was open for 12% -> 11% of each run, Pallas kernels for 0% -> 0%
where the time goes in v1:
time: 210 us
  waiting for transfers between devices  146 us (70%)
  between operations  15.9 us (8%)
  other arithmetic  14.1 us (7%)
  blocking collectives  10.9 us (5%)
  starting transfers between devices  10 us (5%)
  local copies, waits for them, and re-layouts  8.15 us (4%)
  matrix products  4.83 us (2%)
    ppermute x15, waiting for transfers between devices, on_device(): blocks = [lax.ppermute(blocks[0], 'dp', forward), *blocks]  96.8 us
    reduce_scatter x1, waiting for transfers between devices, on_device(): lax.psum_scatter(jnp.dot(attended, w_output, preferred_element_type=jnp.f...  39.8 us
    all_gather x1, blocking collectives, on_device(): gathered = lax.all_gather(activations, 'section', axis=0, tiled=True)  10.9 us
    all_to_all x1, waiting for transfers between devices, on_device(): lax.all_to_all(outgoing_blocks.astype(jnp.bfloat16), 'dp', split_axis=0,...  8.23 us
    all_to_all x1, starting transfers between devices, on_device(): lax.all_to_all(term_rows.astype(jnp.bfloat16), 'dp', split_axis=0, concat...  5.82 us
  transfers between devices with their start and end apart: 19, of which 17 were waited for; matrix products, arithmetic and copies ran while one was open for 11% of the time, Pallas kernels for 0%

profile of v1, /device:TPU:0, one launch (start us, length us, event | category | flops | bytes accessed | tf_op | source)
XLA Modules:
  0.0 209.7 jit_solution(3228997681981851938)
XLA Ops:
  8.0 10.9 %all_gather.3 = bf16[4,16,4608]{2,1,0:T(8,128)(2,1)S(1)} all-gather(bf16[2,16,4608]{2,1,0:T(8,128)(2,1)} %param.12), channel_id=1, replica_groups=mesh['section'=2,'dp'=16] {'section'}, dimensions={0}, use_global_device_ids=true | all-gather | bytes 884736 | tf_op jit(solution)/shard_map/all_gather | solution.py:65
  19.7 7.3 %collective-permute-done = bf16[16,4608]{1,0:T(8,128)(2,1)S(1)} collective-permute-done((bf16[16,4608]{1,0:T(8,128)(2,1)S(1)}, bf16[16,4608]{1,0:T(8,128)(2,1)S(1)}, u32[]{:S(2)}, u32[]{:S(2)}) %collective-permute-start) | collective-permute-done | bytes 147488 | tf_op jit(solution)/shard_map/ppermute | solution.py:96
  27.0 7.3 %collective-permute-done.1 = bf16[16,4608]{1,0:T(8,128)(2,1)S(1)} collective-permute-done((bf16[16,4608]{1,0:T(8,128)(2,1)S(1)}, bf16[16,4608]{1,0:T(8,128)(2,1)S(1)}, u32[]{:S(2)}, u32[]{:S(2)}) %collective-permute-start.1) | collective-permute-done | bytes 147488 | tf_op jit(solution)/shard_map/ppermute | solution.py:96
  34.2 7.3 %collective-permute-done.2 = bf16[16,4608]{1,0:T(8,128)(2,1)S(1)} collective-permute-done((bf16[16,4608]{1,0:T(8,128)(2,1)S(1)}, bf16[16,4608]{1,0:T(8,128)(2,1)S(1)}, u32[]{:S(2)}, u32[]{:S(2)}) %collective-permute-start.2) | collective-permute-done | bytes 147488 | tf_op jit(solution)/shard_map/ppermute | solution.py:96
  41.5 7.3 %collective-permute-done.3 = bf16[16,4608]{1,0:T(8,128)(2,1)S(1)} collective-permute-done((bf16[16,4608]{1,0:T(8,128)(2,1)S(1)}, bf16[16,4608]{1,0:T(8,128)(2,1)S(1)}, u32[]{:S(2)}, u32[]{:S(2)}) %collective-permute-start.3) | collective-permute-done | bytes 147488 | tf_op jit(solution)/shard_map/ppermute | solution.py:96
  48.8 7.3 %collective-permute-done.4 = bf16[16,4608]{1,0:T(8,128)(2,1)S(1)} collective-permute-done((bf16[16,4608]{1,0:T(8,128)(2,1)S(1)}, bf16[16,4608]{1,0:T(8,128)(2,1)S(1)}, u32[]{:S(2)}, u32[]{:S(2)}) %collective-permute-start.4) | collective-permute-done | bytes 147488 | tf_op jit(solution)/shard_map/ppermute | solution.py:96
  56.0 7.3 %collective-permute-done.5 = bf16[16,4608]{1,0:T(8,128)(2,1)S(1)} collective-permute-done((bf16[16,4608]{1,0:T(8,128)(2,1)S(1)}, bf16[16,4608]{1,0:T(8,128)(2,1)S(1)}, u32[]{:S(2)}, u32[]{:S(2)}) %collective-permute-start.5) | collective-permute-done | bytes 147488 | tf_op jit(solution)/shard_map/ppermute | solution.py:96
  63.3 7.3 %collective-permute-done.6 = bf16[16,4608]{1,0:T(8,128)(2,1)S(1)} collective-permute-done((bf16[16,4608]{1,0:T(8,128)(2,1)S(1)}, bf16[16,4608]{1,0:T(8,128)(2,1)S(1)}, u32[]{:S(2)}, u32[]{:S(2)}) %collective-permute-start.6) | collective-permute-done | bytes 147488 | tf_op jit(solution)/shard_map/ppermute | solution.py:96
  70.5 7.3 %collective-permute-done.7 = bf16[16,4608]{1,0:T(8,128)(2,1)S(1)} collective-permute-done((bf16[16,4608]{1,0:T(8,128)(2,1)S(1)}, bf16[16,4608]{1,0:T(8,128)(2,1)S(1)}, u32[]{:S(2)}, u32[]{:S(2)}) %collective-permute-start.7) | collective-permute-done | bytes 147488 | tf_op jit(solution)/shard_map/ppermute | solution.py:96
  77.8 7.3 %collective-permute-done.8 = bf16[16,4608]{1,0:T(8,128)(2,1)S(1)} collective-permute-done((bf16[16,4608]{1,0:T(8,128)(2,1)S(1)}, bf16[16,4608]{1,0:T(8,128)(2,1)S(1)}, u32[]{:S(2)}, u32[]{:S(2)}) %collective-permute-start.8) | collective-permute-done | bytes 147488 | tf_op jit(solution)/shard_map/ppermute | solution.py:96
  85.1 7.3 %collective-permute-done.9 = bf16[16,4608]{1,0:T(8,128)(2,1)S(1)} collective-permute-done((bf16[16,4608]{1,0:T(8,128)(2,1)S(1)}, bf16[16,4608]{1,0:T(8,128)(2,1)S(1)}, u32[]{:S(2)}, u32[]{:S(2)}) %collective-permute-start.9) | collective-permute-done | bytes 147488 | tf_op jit(solution)/shard_map/ppermute | solution.py:96
  92.3 7.3 %collective-permute-done.10 = bf16[16,4608]{1,0:T(8,128)(2,1)S(1)} collective-permute-done((bf16[16,4608]{1,0:T(8,128)(2,1)S(1)}, bf16[16,4608]{1,0:T(8,128)(2,1)S(1)}, u32[]{:S(2)}, u32[]{:S(2)}) %collective-permute-start.10) | collective-permute-done | bytes 147488 | tf_op jit(solution)/shard_map/ppermute | solution.py:96
  100.9 5.8 %all-to-all-start.1 = ((bf16[16,1,1]{2,1,0:T(2,128)(2,1)}), bf16[16,1,1]{2,1,0:T(2,128)(2,1)S(1)}, u32[]{:S(2)}, u32[]{:S(2)}) async-start(bf16[16,1,1]{2,1,0:T(2,128)(2,1)} %broadcast_in_dim.70), calls=%async_computation.1 | async-start | bytes 16384 | tf_op jit(solution)/shard_map/all_to_all | solution.py:79
  109.4 5.5 %collective-permute-done.12 = bf16[16,4608]{1,0:T(8,128)(2,1)S(1)} collective-permute-done((bf16[16,4608]{1,0:T(8,128)(2,1)S(1)}, bf16[16,4608]{1,0:T(8,128)(2,1)S(1)}, u32[]{:S(2)}, u32[]{:S(2)}) %collective-permute-start.12) | collective-permute-done | bytes 147488 | tf_op jit(solution)/shard_map/ppermute | solution.py:96
  114.8 1.3 fusion.53
  116.1 6.0 %collective-permute-done.13 = bf16[16,4608]{1,0:T(8,128)(2,1)S(1)} collective-permute-done((bf16[16,4608]{1,0:T(8,128)(2,1)S(1)}, bf16[16,4608]{1,0:T(8,128)(2,1)S(1)}, u32[]{:S(2)}, u32[]{:S(2)}) %collective-permute-start.13) | collective-permute-done | bytes 147488 | tf_op jit(solution)/shard_map/ppermute | solution.py:96
  122.7 1.4 reduce.1
  124.0 5.4 %collective-permute-done.14 = bf16[16,4608]{1,0:T(8,128)(2,1)} collective-permute-done((bf16[16,4608]{1,0:T(8,128)(2,1)S(1)}, bf16[16,4608]{1,0:T(8,128)(2,1)}, u32[]{:S(2)}, u32[]{:S(2)}) %collective-permute-start.14) | collective-permute-done | bytes 147488 | tf_op jit(solution)/shard_map/ppermute | solution.py:96
  136.8 2.4 %convolution_convert_fusion = bf16[256,4608]{1,0:T(8,128)(2,1)} fusion(bf16[1,128,4608]{2,1,0:T(8,128)(2,1)S(1)} %copy-done, bf16[256,256]{0,1:T(8,128)(2,1)S(1)} %get-tuple-element.20, f32[256]{0:T(256)S(1)} %get-tuple-element.19, bf16[256,128]{0,1:T(8,128)(2,1)S(1)} %collective-permute-done.15, bf16[256,128]{0,1:T(8,128)(2,1)S(1)} %fusion.20, pred[]{:T(512)S(6)} %eq.34), kind=kOutput, calls=%fused_computation.4 | convolution fusion | flops 320045056 | bytes 3802113 | tf_op jit(solution)/shard_map/dot_general | solution.py:131
  143.6 3.6 %all-to-all-start = ((bf16[16,2,4608]{2,1,0:T(2,128)(2,1)}), bf16[16,2,4608]{2,1,0:T(2,128)(2,1)S(1)}, u32[]{:S(2)}, u32[]{:S(2)}) async-start(bf16[16,2,4608]{2,1,0:T(2,128)(2,1)} %select_convert_fusion), calls=%async_computation | async-start | bytes 589824 | tf_op jit(solution)/shard_map/all_to_all | solution.py:76
  149.5 8.2 %all-to-all-done = bf16[16,2,4608]{2,1,0:T(2,128)(2,1)S(1)} async-done(((bf16[16,2,4608]{2,1,0:T(2,128)(2,1)}), bf16[16,2,4608]{2,1,0:T(2,128)(2,1)S(1)}, u32[]{:S(2)}, u32[]{:S(2)}) %all-to-all-start) | async-done | bytes 294944 | tf_op jit(solution)/shard_map/all_to_all | solution.py:76
  157.9 1.2 gather_fusion.3
  160.2 39.8 %reduce-scatter.2.cloned.1.call-done = bf16[16,4608]{1,0:T(8,128)(2,1)} async-done(((bf16[256,4608]{1,0:T(8,128)(2,1)}), bf16[16,4608]{1,0:T(8,128)(2,1)}) %reduce-scatter.2.cloned.1.call-update) | async-done | bytes 147472 | tf_op jit(solution)/shard_map/reduce_scatter | solution.py:130
  201.1 1.7 fusion.19
  (112 shorter events, 20.7 us)
Async XLA Ops:
  7.2 129.6 %copy-start = (bf16[1,128,4608]{2,1,0:T(8,128)(2,1)S(1)}, bf16[1,128,4608]{2,1,0:T(8,128)(2,1)}, u32[]{:S(2)}) copy-start(bf16[1,128,4608]{2,1,0:T(8,128)(2,1)} %param.20) | copy-start | bytes 3538948
  19.6 181.5 %copy-start.1 = (bf16[2,16,4608]{2,1,0:T(8,128)(2,1)}, bf16[2,16,4608]{2,1,0:T(8,128)(2,1)S(1)}, u32[]{:S(2)}) copy-start(bf16[2,16,4608]{2,1,0:T(8,128)(2,1)S(1)} %broadcast_select_fusion) | copy-start | bytes 884740
  19.6 7.3 %collective-permute-start = (bf16[16,4608]{1,0:T(8,128)(2,1)S(1)}, bf16[16,4608]{1,0:T(8,128)(2,1)S(1)}, u32[]{:S(2)}, u32[]{:S(2)}) collective-permute-start(bf16[16,4608]{1,0:T(8,128)(2,1)S(1)} %slice_bitcast_fusion), channel_id=1, source_target_pairs={{0,1},{1,2},{2,3},{3,4},{4,5},{5,6},{6,7},{7,8},{8,9},{9,10},{10,1... | collective-permute-start | bytes 442376 | tf_op jit(solution)/shard_map/ppermute | solution.py:96
  27.0 7.3 %collective-permute-start.1 = (bf16[16,4608]{1,0:T(8,128)(2,1)S(1)}, bf16[16,4608]{1,0:T(8,128)(2,1)S(1)}, u32[]{:S(2)}, u32[]{:S(2)}) collective-permute-start(bf16[16,4608]{1,0:T(8,128)(2,1)S(1)} %collective-permute-done), channel_id=1, source_target_pairs={{0,1},{1,2},{2,3},{3,4},{4,5},{5,6},{6,7},{7,8},{8,9},{9,10},{10,1... | collective-permute-start | bytes 442376 | tf_op jit(solution)/shard_map/ppermute | solution.py:96
  34.2 7.3 %collective-permute-start.2 = (bf16[16,4608]{1,0:T(8,128)(2,1)S(1)}, bf16[16,4608]{1,0:T(8,128)(2,1)S(1)}, u32[]{:S(2)}, u32[]{:S(2)}) collective-permute-start(bf16[16,4608]{1,0:T(8,128)(2,1)S(1)} %collective-permute-done.1), channel_id=1, source_target_pairs={{0,1},{1,2},{2,3},{3,4},{4,5},{5,6},{6,7},{7,8},{8,9},{9,10},{10,1... | collective-permute-start | bytes 442376 | tf_op jit(solution)/shard_map/ppermute | solution.py:96
  41.5 7.3 %collective-permute-start.3 = (bf16[16,4608]{1,0:T(8,128)(2,1)S(1)}, bf16[16,4608]{1,0:T(8,128)(2,1)S(1)}, u32[]{:S(2)}, u32[]{:S(2)}) collective-permute-start(bf16[16,4608]{1,0:T(8,128)(2,1)S(1)} %collective-permute-done.2), channel_id=1, source_target_pairs={{0,1},{1,2},{2,3},{3,4},{4,5},{5,6},{6,7},{7,8},{8,9},{9,10},{10,1... | collective-permute-start | bytes 442376 | tf_op jit(solution)/shard_map/ppermute | solution.py:96
  48.7 7.3 %collective-permute-start.4 = (bf16[16,4608]{1,0:T(8,128)(2,1)S(1)}, bf16[16,4608]{1,0:T(8,128)(2,1)S(1)}, u32[]{:S(2)}, u32[]{:S(2)}) collective-permute-start(bf16[16,4608]{1,0:T(8,128)(2,1)S(1)} %collective-permute-done.3), channel_id=1, source_target_pairs={{0,1},{1,2},{2,3},{3,4},{4,5},{5,6},{6,7},{7,8},{8,9},{9,10},{10,1... | collective-permute-start | bytes 442376 | tf_op jit(solution)/shard_map/ppermute | solution.py:96
  56.0 7.3 %collective-permute-start.5 = (bf16[16,4608]{1,0:T(8,128)(2,1)S(1)}, bf16[16,4608]{1,0:T(8,128)(2,1)S(1)}, u32[]{:S(2)}, u32[]{:S(2)}) collective-permute-start(bf16[16,4608]{1,0:T(8,128)(2,1)S(1)} %collective-permute-done.4), channel_id=1, source_target_pairs={{0,1},{1,2},{2,3},{3,4},{4,5},{5,6},{6,7},{7,8},{8,9},{9,10},{10,1... | collective-permute-start | bytes 442376 | tf_op jit(solution)/shard_map/ppermute | solution.py:96
  63.3 7.3 %collective-permute-start.6 = (bf16[16,4608]{1,0:T(8,128)(2,1)S(1)}, bf16[16,4608]{1,0:T(8,128)(2,1)S(1)}, u32[]{:S(2)}, u32[]{:S(2)}) collective-permute-start(bf16[16,4608]{1,0:T(8,128)(2,1)S(1)} %collective-permute-done.5), channel_id=1, source_target_pairs={{0,1},{1,2},{2,3},{3,4},{4,5},{5,6},{6,7},{7,8},{8,9},{9,10},{10,1... | collective-permute-start | bytes 442376 | tf_op jit(solution)/shard_map/ppermute | solution.py:96
  70.5 7.3 %collective-permute-start.7 = (bf16[16,4608]{1,0:T(8,128)(2,1)S(1)}, bf16[16,4608]{1,0:T(8,128)(2,1)S(1)}, u32[]{:S(2)}, u32[]{:S(2)}) collective-permute-start(bf16[16,4608]{1,0:T(8,128)(2,1)S(1)} %collective-permute-done.6), channel_id=1, source_target_pairs={{0,1},{1,2},{2,3},{3,4},{4,5},{5,6},{6,7},{7,8},{8,9},{9,10},{10,1... | collective-permute-start | bytes 442376 | tf_op jit(solution)/shard_map/ppermute | solution.py:96
  77.8 7.3 %collective-permute-start.8 = (bf16[16,4608]{1,0:T(8,128)(2,1)S(1)}, bf16[16,4608]{1,0:T(8,128)(2,1)S(1)}, u32[]{:S(2)}, u32[]{:S(2)}) collective-permute-start(bf16[16,4608]{1,0:T(8,128)(2,1)S(1)} %collective-permute-done.7), channel_id=1, source_target_pairs={{0,1},{1,2},{2,3},{3,4},{4,5},{5,6},{6,7},{7,8},{8,9},{9,10},{10,1... | collective-permute-start | bytes 442376 | tf_op jit(solution)/shard_map/ppermute | solution.py:96
  85.1 7.3 %collective-permute-start.9 = (bf16[16,4608]{1,0:T(8,128)(2,1)S(1)}, bf16[16,4608]{1,0:T(8,128)(2,1)S(1)}, u32[]{:S(2)}, u32[]{:S(2)}) collective-permute-start(bf16[16,4608]{1,0:T(8,128)(2,1)S(1)} %collective-permute-done.8), channel_id=1, source_target_pairs={{0,1},{1,2},{2,3},{3,4},{4,5},{5,6},{6,7},{7,8},{8,9},{9,10},{10,1... | collective-permute-start | bytes 442376 | tf_op jit(solution)/shard_map/ppermute | solution.py:96
  92.3 7.3 %collective-permute-start.10 = (bf16[16,4608]{1,0:T(8,128)(2,1)S(1)}, bf16[16,4608]{1,0:T(8,128)(2,1)S(1)}, u32[]{:S(2)}, u32[]{:S(2)}) collective-permute-start(bf16[16,4608]{1,0:T(8,128)(2,1)S(1)} %collective-permute-done.9), channel_id=1, source_target_pairs={{0,1},{1,2},{2,3},{3,4},{4,5},{5,6},{6,7},{7,8},{8,9},{9,10},{10,1... | collective-permute-start | bytes 442376 | tf_op jit(solution)/shard_map/ppermute | solution.py:96
  99.6 7.9 %collective-permute-start.11 = (bf16[16,4608]{1,0:T(8,128)(2,1)S(1)}, bf16[16,4608]{1,0:T(8,128)(2,1)S(1)}, u32[]{:S(2)}, u32[]{:S(2)}) collective-permute-start(bf16[16,4608]{1,0:T(8,128)(2,1)S(1)} %collective-permute-done.10), channel_id=1, source_target_pairs={{0,1},{1,2},{2,3},{3,4},{4,5},{5,6},{6,7},{7,8},{8,9},{9,10},{10,1... | collective-permute-start | bytes 442376 | tf_op jit(solution)/shard_map/ppermute | solution.py:96
  100.9 42.7 %all-to-all-start.1 = ((bf16[16,1,1]{2,1,0:T(2,128)(2,1)}), bf16[16,1,1]{2,1,0:T(2,128)(2,1)S(1)}, u32[]{:S(2)}, u32[]{:S(2)}) async-start(bf16[16,1,1]{2,1,0:T(2,128)(2,1)} %broadcast_in_dim.70), calls=%async_computation.1 | async-start | bytes 16384 | tf_op jit(solution)/shard_map/all_to_all | solution.py:79
  106.7 93.4 %reduce-scatter.2.cloned.1.call-start = ((), (), s32[]{:S(2)}) async-start(), calls=%async_computation.3 | async-start | bytes 2506752 | tf_op jit(solution)/shard_map/reduce_scatter | solution.py:130
  107.5 7.3 %collective-permute-start.12 = (bf16[16,4608]{1,0:T(8,128)(2,1)S(1)}, bf16[16,4608]{1,0:T(8,128)(2,1)S(1)}, u32[]{:S(2)}, u32[]{:S(2)}) collective-permute-start(bf16[16,4608]{1,0:T(8,128)(2,1)S(1)} %collective-permute-done.11), channel_id=1, source_target_pairs={{0,1},{1,2},{2,3},{3,4},{4,5},{5,6},{6,7},{7,8},{8,9},{9,10},{10,1... | collective-permute-start | bytes 442376 | tf_op jit(solution)/shard_map/ppermute | solution.py:96
  114.8 7.3 %collective-permute-start.13 = (bf16[16,4608]{1,0:T(8,128)(2,1)S(1)}, bf16[16,4608]{1,0:T(8,128)(2,1)S(1)}, u32[]{:S(2)}, u32[]{:S(2)}) collective-permute-start(bf16[16,4608]{1,0:T(8,128)(2,1)S(1)} %collective-permute-done.12), channel_id=1, source_target_pairs={{0,1},{1,2},{2,3},{3,4},{4,5},{5,6},{6,7},{7,8},{8,9},{9,10},{10,1... | collective-permute-start | bytes 442376 | tf_op jit(solution)/shard_map/ppermute | solution.py:96
  122.1 7.4 %collective-permute-start.14 = (bf16[16,4608]{1,0:T(8,128)(2,1)S(1)}, bf16[16,4608]{1,0:T(8,128)(2,1)}, u32[]{:S(2)}, u32[]{:S(2)}) collective-permute-start(bf16[16,4608]{1,0:T(8,128)(2,1)S(1)} %collective-permute-done.13), channel_id=1, source_target_pairs={{0,1},{1,2},{2,3},{3,4},{4,5},{5,6},{6,7},{7,8},{8,9},{9,10},{10,1... | collective-permute-start | bytes 442376 | tf_op jit(solution)/shard_map/ppermute | solution.py:96
  134.8 4.4 %copy-start.6 = (s32[16,1,1]{0,2,1:T(1,128)S(1)}, s32[16,1,1]{0,2,1:T(1,128)}, u32[]{:S(2)}) copy-start(s32[16,1,1]{0,2,1:T(1,128)} %fusion.53) | copy-start | bytes 196
  134.8 5.8 %copy-start.2 = (f32[16,2,4608]{2,1,0:T(2,128)S(1)}, f32[16,2,4608]{2,1,0:T(2,128)}, u32[]{:S(2)}) copy-start(f32[16,2,4608]{2,1,0:T(2,128)} %param.14) | copy-start | bytes 1769476
  134.8 8.7 %copy-start.4 = (f32[1,4608]{1,0:T(1,128)S(1)}, f32[1,4608]{1,0:T(1,128)}, u32[]{:S(2)}) copy-start(f32[1,4608]{1,0:T(1,128)} %param.21) | copy-start | bytes 55300
  135.2 1.3 collective-permute-start.15
  143.6 14.1 %all-to-all-start = ((bf16[16,2,4608]{2,1,0:T(2,128)(2,1)}), bf16[16,2,4608]{2,1,0:T(2,128)(2,1)S(1)}, u32[]{:S(2)}, u32[]{:S(2)}) async-start(bf16[16,2,4608]{2,1,0:T(2,128)(2,1)} %select_convert_fusion), calls=%async_computation | async-start | bytes 589824 | tf_op jit(solution)/shard_map/all_to_all | solution.py:76
  (4 other events, 8.1 us)
Sparse Core Ops, SparseCore 0:
  139.3 60.6 reduce-scatter.1
